TPU v7x, 32 devices: a whole 2x2x4 slice. The times are simulated.
32 devices in a mesh: seq: 8 (over z, y), batch: 4 (over x, core).
Axes of the slice: x: 2, y: 2, z: 4, core: 2. Of those that a mesh axis runs over, the one named last changes fastest.
Arguments:
- queries: bfloat16 [4, 1024, 4096], P('batch', 'seq'), may hold values from -130 to 130
- keys: bfloat16 [4, 1024, 1024], P('batch', 'seq'), may hold values from -4 to 4
- values: bfloat16 [4, 1024, 1024], P('batch', 'seq'), may hold values from -4 to 4
- lengths: int32 [4], P('batch'), may hold values from 512 to 1024
- block_pos: int32 [4, 8], P('batch'), may hold values from 0 to 7, each once within a row
- w_in: bfloat16 [6144, 1024], replicated, may hold values from -0.078125 to 0.078125
- b_in: float32 [1024], replicated, may hold values from -3 to 3
- output_weight: bfloat16 [1024, 8], replicated, may hold values from -0.1875 to 0.1875
- output_bias: float32 [8], replicated, may hold values from 1 to 2
Outputs:
- grad_w_in: float32 [6144, 1024], P(('seq', 'batch'))
- grad_b_in: float32 [1024], replicated
- output_weight_gradient: float32 [1024, 8], replicated
- output_bias_gradient: float32 [8], replicated
Inputs may be any that keep to these rules, and one draw needn't show every extreme that they name: Each row of block_pos names every block 0 to 7 once.
All inputs are finite; a program needn't handle non-finite values.
Results may differ from a plain program's by a relative error of at most 0.0017.
The roundings to bfloat16 on the way count: a program that leaves them out, or rounds other values in their place, can miss the bound.
Values may be sent and summed in bfloat16 or wider, within the bound.
A program may use at most 128 MiB of HBM per device.

v0:
```python
import math

import jax
import jax.numpy as jnp
from jax import lax
from jax.sharding import PartitionSpec as P


def on_device(queries, keys, values, lengths, block_pos, w_in, b_in, output_weight, output_bias):
    q_rows = queries[0]
    k_rows = keys[0]
    v_rows = values[0]
    rows = q_rows.shape[0]
    heads_kv = output_weight.shape[1]
    head_size = k_rows.shape[1] // heads_kv
    group_index = q_rows.shape[1] // k_rows.shape[1]
    scale = 1.0 / math.sqrt(head_size)
    every_key = lax.all_gather(k_rows, "seq", axis=0, tiled=True)
    total = every_key.shape[0]
    order = block_pos[0]
    offsets = jnp.arange(rows, dtype=jnp.int32)
    key_pos = (order[:, None] * rows + offsets[None, :]).reshape(-1)
    mine = lax.axis_index("seq")
    query_pos = lax.dynamic_index_in_dim(order, mine, 0, keepdims=False) * rows + offsets
    limit = lengths[0]
    allowed = (key_pos[None, :] <= query_pos[:, None]) & (key_pos < limit)[None, :]
    query_live = (query_pos < limit).astype(jnp.float32)

    def group_mass(index, sums):
        q_part = lax.dynamic_slice_in_dim(
            q_rows, index * group_index * head_size, group_index * head_size, 1
        )
        q_part = q_part.reshape(rows, group_index, head_size)
        k_part = lax.dynamic_slice_in_dim(every_key, index * head_size, head_size, 1)
        scores = (
            jnp.einsum("qhd,kd->hqk", q_part, k_part, preferred_element_type=jnp.float32) * scale
        )
        masked = jnp.where(allowed[None], scores, -1e30)
        top = jnp.max(masked, axis=2, keepdims=True)
        weights = jnp.where(allowed[None], jnp.exp(masked - top), 0.0)
        denom = jnp.sum(weights, axis=2, keepdims=True)
        share = weights / denom * query_live[None, :, None]
        column = jnp.sum(share, axis=(0, 1))
        return lax.dynamic_update_index_in_dim(sums, column, index, 0)

    partial_value = lax.fori_loop(
        0, heads_kv, group_mass, jnp.zeros((heads_kv, total), jnp.float32)
    )
    mass = lax.psum_scatter(partial_value, "seq", scatter_dimension=1, tiled=True)
    labels = jnp.log1p(mass).T
    features = jnp.concatenate([q_rows, k_rows, v_rows], axis=1)
    pre = jnp.dot(features, w_in, preferred_element_type=jnp.float32) + b_in
    act = jax.nn.silu(pre).astype(jnp.bfloat16)
    pred = jnp.dot(act, output_weight, preferred_element_type=jnp.float32) + output_bias
    norm = 1.0 / math.sqrt(lax.axis_size("batch") * total)
    resid = ((pred - labels) * query_live[:, None] * norm).astype(jnp.bfloat16)
    back = lax.dot_general(
        resid, output_weight, (((1,), (1,)), ((), ())), preferred_element_type=jnp.float32
    )
    sig = jax.nn.sigmoid(pre)
    delta = (back * sig * (1.0 + pre * (1.0 - sig))).astype(jnp.bfloat16)
    out_term = lax.dot_general(
        act, resid, (((0,), (0,)), ((), ())), preferred_element_type=jnp.float32
    )
    grad_b_in, output_weight_gradient, output_bias_gradient = lax.psum(
        (
            jnp.sum(delta.astype(jnp.float32), axis=0),
            out_term,
            jnp.sum(resid.astype(jnp.float32), axis=0),
        ),
        ("seq", "batch"),
    )
    term = lax.dot_general(
        features, delta, (((0,), (0,)), ((), ())), preferred_element_type=jnp.float32
    )
    grad_w_in = lax.psum_scatter(term, ("seq", "batch"), scatter_dimension=0, tiled=True)
    return (grad_w_in, grad_b_in, output_weight_gradient, output_bias_gradient)


def solution(mesh):
    return jax.shard_map(
        on_device,
        mesh=mesh,
        in_specs=(
            P("batch", "seq", None),
            P("batch", "seq", None),
            P("batch", "seq", None),
            P("batch"),
            P("batch", None),
            P(),
            P(),
            P(),
            P(),
        ),
        out_specs=(P(("seq", "batch"), None), P(), P(), P()),
        check_vma=False,
    )
```

profile of v0, /device:TPU:0, one launch (start us, length us, event | category | flops | bytes accessed | tf_op | source)
XLA Modules:
  0.0 454.6 jit_solution(4528284244883163602)
XLA Ops:
  10.9 1.6 copy.14
  13.9 6.5 %multiply_convert_fusion = (bf16[128,1024]{1,0:T(8,128)(2,1)S(1)}, f32[128,1024]{1,0:T(8,128)S(1)}) fusion(f32[1024]{0:T(1024)S(1)} %copy-done.1, bf16[6144,1024]{1,0:T(8,128)(2,1)} %param.16, bf16[128,1024]{0,1:T(8,128)(2,1)S(1)} %bitcast.76, bf16[128,1024]{0,1:T(8,128)(2,1)S(1)} %bitcast.74, bf16[128,4096]{0,1:T(8,128)(2,1)S(1)} %bitcast.70), kind=kOutput, calls=%fused_computation.38 | convolution fusion | flops 1616117760 | bytes 14946304 | tf_op jit(solution)/shard_map/dot_general | solution.py:52
  20.4 41.6 %all-gather.3.cloned.1.call-done = bf16[1,1024,1024]{2,1,0:T(8,128)(2,1)} async-done(((bf16[1,128,1024]{2,1,0:T(8,128)(2,1)}), bf16[1,1024,1024]{2,1,0:T(8,128)(2,1)}) %all-gather.3.cloned.1.call-update) | async-done | bytes 2097168 | tf_op jit(solution)/shard_map/all_gather | solution.py:18
  62.0 75.7 %while.16 = (s32[]{:T(128)}, f32[8,1024]{1,0:T(8,128)}, bf16[1024,1024]{1,0:T(8,128)(2,1)}, bf16[128,4096]{0,1:T(8,128)(2,1)S(1)}, s32[128]{0:T(128)S(1)}, /*ind...) while((s32[]{:T(128)}, f32[8,1024]{1,0:T(8,128)}, ...), condition=%wide.region_4.5_spmd.clone, body=%wide.region_0.4_spmd.clone.sunk | while | flops 274468736 | bytes 5917449 | solution.py:46
  63.7 3.4 fusion.71
  67.1 3.0 multiply_reduce_fusion.2
  70.1 1.4 dynamic_update_slice.13
  73.1 3.4 fusion.71
  76.6 3.0 multiply_reduce_fusion.2
  79.5 1.4 dynamic_update_slice.13
  82.6 3.4 fusion.71
  86.0 3.0 multiply_reduce_fusion.2
  89.0 1.4 dynamic_update_slice.13
  92.1 3.4 fusion.71
  95.5 3.0 multiply_reduce_fusion.2
  98.4 1.4 dynamic_update_slice.13
  101.5 3.4 fusion.71
  104.9 3.0 multiply_reduce_fusion.2
  107.9 1.4 dynamic_update_slice.13
  111.0 3.4 fusion.71
  114.4 3.0 multiply_reduce_fusion.2
  117.4 1.4 dynamic_update_slice.13
  120.4 3.4 fusion.71
  123.8 3.0 multiply_reduce_fusion.2
  126.8 1.4 dynamic_update_slice.13
  129.9 3.4 fusion.71
  133.3 3.0 multiply_reduce_fusion.2
  136.3 1.4 dynamic_update_slice.13
  138.4 52.8 %reduce-scatter.3.cloned.1.call-done = f32[8,128]{1,0:T(8,128)} async-done(((f32[8,1024]{1,0:T(8,128)}), f32[8,128]{1,0:T(8,128)}) %reduce-scatter.3.cloned.1.call-update) | async-done | bytes 4112 | tf_op jit(solution)/shard_map/reduce_scatter | solution.py:49
  192.5 13.2 %fusion.45 = f32[6144,1024]{1,0:T(8,128)} fusion(bf16[128,1024]{1,0:T(8,128)(2,1)S(1)} %get-tuple-element.209, bf16[128,1024]{0,1:T(8,128)(2,1)S(1)} %bitcast.77, bf16[128,1024]{0,1:T(8,128)(2,1)S(1)} %bitcast.75, bf16[128,4096]{0,1:T(8,128)(2,1)S(1)} %get-tuple-element.317), kind=kOutput, calls=%fused_computation.36 | convolution fusion | flops 1615331328 | bytes 27000832 | tf_op jit(solution)/shard_map/dot_general | solution.py:73
  205.9 41.0 %all-reduce = (f32[1024]{0:T(1024)}, f32[1024,8]{0,1:T(8,128)}, f32[8]{0:T(128)}) all-reduce(f32[1024]{0:T(1024)S(1)} %get-tuple-element.208, f32[1024,8]{0,1:T(8,128)S(1)} %fusion.51, f32[8]{0:T(128)S(1)} %get-tuple-element.210), channel_id=1, replica_groups=mesh['seq'=8,'batch'=4] {'seq','batch'}, use_global_device_ids=true, to_apply=%region_8.9 | all-reduce | flops 9224 | bytes 73792 | tf_op jit(solution)/shard_map/psum | solution.py:65
  246.9 201.1 %reduce-scatter.5.cloned.1.call-done = f32[192,1024]{1,0:T(8,128)} async-done(((f32[6144,1024]{1,0:T(8,128)}), f32[192,1024]{1,0:T(8,128)}) %reduce-scatter.5.cloned.1.call-update) | async-done | bytes 786448 | tf_op jit(solution)/shard_map/reduce_scatter | solution.py:76
  (50 shorter events, 19.8 us)
Async XLA Ops:
  7.2 184.0 %copy-start = (bf16[1024,8]{0,1:T(8,128)(2,1)S(1)}, bf16[1024,8]{0,1:T(8,128)(2,1)}, u32[]{:S(2)}) copy-start(bf16[1024,8]{0,1:T(8,128)(2,1)} %param.18) | copy-start | bytes 49156
  7.2 5.3 %copy-start.2 = (s32[1,8]{1,0:T(1,128)S(1)}, s32[1,8]{1,0:T(1,128)}, u32[]{:S(2)}) copy-start(s32[1,8]{1,0:T(1,128)} %param.15) | copy-start | bytes 100
  7.2 6.8 %copy-start.1 = (f32[1024]{0:T(1024)S(1)}, f32[1024]{0:T(1024)}, u32[]{:S(2)}) copy-start(f32[1024]{0:T(1024)} %param.17) | copy-start | bytes 12292
  7.2 54.8 %all-gather.3.cloned.1.call-start = ((), (), s32[]{:S(2)}) async-start(), calls=%async_computation.4 | async-start | bytes 2359296 | tf_op jit(solution)/shard_map/all_gather | solution.py:18
  7.9 183.2 %reduce-scatter.3.cloned.1.call-start = ((), (), s32[]{:S(2)}) async-start(), calls=%async_computation.2 | async-start | bytes 36864 | tf_op jit(solution)/shard_map/reduce_scatter | solution.py:49
  62.0 129.2 %copy-start.3 = (f32[8]{0:T(128)S(1)}, f32[8]{0:T(128)}, u32[]{:S(2)}) copy-start(f32[8]{0:T(128)} %param.19) | copy-start | bytes 100
  137.7 310.3 %reduce-scatter.5.cloned.1.call-start = ((), (), s32[]{:S(2)}) async-start(), calls=%async_computation.3 | async-start | bytes 25952256 | tf_op jit(solution)/shard_map/reduce_scatter | solution.py:76
Sparse Core Ops, SparseCore 0:
  10.1 51.8 all-gather.2
  137.8 53.3 reduce-scatter.2
  205.9 242.0 reduce-scatter.4
where the time goes:
time: 456 us; the launch traced here: 455 us
  waiting for transfers between devices  296 us (65%)
  matrix products  72.3 us (16%)
  blocking collectives  41 us (9%)
  local copies, waits for them, and re-layouts  15.2 us (3%)
  other arithmetic  15.1 us (3%)
  between operations  14.5 us (3%)
    reduce_scatter x1, waiting for transfers between devices, on_device(): lax.psum_scatter(term, ('seq', 'batch'), scatter_dimension=0, tiled=True)  201 us
    reduce_scatter x1, waiting for transfers between devices, on_device(): lax.psum_scatter(partial_value, 'seq', scatter_dimension=1, tiled=True)  52.8 us
    all_gather x1, waiting for transfers between devices, on_device(): every_key = lax.all_gather(k_rows, 'seq', axis=0, tiled=True)  41.6 us
    psum x1, blocking collectives, on_device(): lax.psum((jnp.sum(delta.astype(jnp.float32), axis=0), out_term, jnp.sum(r...  41 us
    div x8, matrix products, group_mass(): share = weights / denom * query_live[None, :, None]  27.3 us
    sub x8, matrix products, group_mass(): weights = jnp.where(allowed[None], jnp.exp(masked - top), 0.0)  23.8 us
    dot_general x1, matrix products, on_device(): lax.dot_general(features, delta, (((0,), (0,)), ((), ())), preferred_elem...  13.2 us
    dynamic_update_slice x8, local copies, waits for them, and re-layouts, group_mass(): return lax.dynamic_update_index_in_dim(sums, column, index, 0)  11.2 us
  transfers between devices with their start and end apart: 3, of which 3 were waited for; matrix products, arithmetic and copies ran while one was open for 3% of the time, Pallas kernels for 0%

commit v1 on v0

v1 whole, which is shorter than its diff:
```python
import functools
import math

import jax
import jax.numpy as jnp
from jax import lax
from jax.experimental import pallas as pl
from jax.experimental.pallas import tpu as pltpu
from jax.sharding import PartitionSpec as P

F32 = jnp.float32
BF16 = jnp.bfloat16
MESH = pl.DeviceIdType.MESH


def copy_to(src, dst, send, recv, target):
    return pltpu.make_async_remote_copy(
        src_ref=src,
        dst_ref=dst,
        send_sem=send,
        recv_sem=recv,
        device_id=target,
        device_id_type=MESH,
    )


def kernel(
    n,
    nb,
    norm,
    scale,
    q_ref,
    k_ref,
    feat_ref,
    pre_ref,
    wt_ref,
    bias_ref,
    kpos_ref,
    qpos_ref,
    live_col_ref,
    live_row_ref,
    limit_ref,
    grad_ref,
    gb_ref,
    gw_ref,
    kg,
    ft,
    act,
    msum,
    mp,
    mr,
    delta,
    dg,
    otc,
    otr,
    obs,
    obr,
    ofin,
    dbs,
    dbr,
    cs,
    cr,
    ksem,
    fsem,
    msem,
    dsem,
    osem,
    bsem,
    gsem,
    hsem,
    csem,
):
    me = lax.axis_index("seq")
    mb = lax.axis_index("batch")
    rows, kd = k_ref.shape
    heads = msum.shape[0]
    head = kd // heads
    per_group = q_ref.shape[1] // kd
    hidden = pre_ref.shape[1]
    inner = 2
    outer = n // inner
    mo = me // inner
    mi = me % inner
    pair = mo * inner + (inner - 1 - mi)

    def seq_peer(d):
        return lax.rem(me + d, n)

    def batch_peer(d):
        return lax.rem(mb + d, nb)

    def outer_peer(d):
        return lax.rem(mo + d, outer) * inner + mi

    def outer_source(d):
        return lax.rem(mo - d + outer, outer) * inner + mi

    barrier = pltpu.get_barrier_semaphore()
    for d in range(1, n):
        pl.semaphore_signal(barrier, inc=1, device_id={"seq": seq_peer(d)}, device_id_type=MESH)
    for d in range(1, nb):
        pl.semaphore_signal(
            barrier, inc=1, device_id={"batch": batch_peer(d)}, device_id_type=MESH
        )
    pl.semaphore_wait(barrier, n + nb - 2)

    def block(ref, owner):
        return ref.at[pl.ds(pl.multiple_of(owner * rows, rows), rows)]

    def gather_start(src, dst, sem):
        copies = []
        for d in range(1, outer):
            copy = copy_to(
                src, block(dst, me), sem.at[0, d], sem.at[1, d], {"seq": outer_peer(d)}
            )
            copy.start()
            copies.append(copy)
        copy = copy_to(src, block(dst, me), sem.at[2, 0], sem.at[3, 0], {"seq": pair})
        copy.start()
        return copies, [copy]

    def gather_finish(dst, sem, started):
        direct, passed = started
        for d in range(1, outer):
            direct[d - 1].wait_recv()
            held = block(dst, outer_source(d))
            copy = copy_to(held, held, sem.at[2, d], sem.at[3, d], {"seq": pair})
            copy.start()
            passed.append(copy)
        for copy in passed:
            copy.wait_recv()
        return direct + passed

    key_copies = gather_start(k_ref, kg, ksem)
    feat_copies = []
    for d in range(1, n):
        copy = copy_to(
            feat_ref.at[seq_peer(d)],
            ft.at[:, pl.ds(pl.multiple_of(me * rows, rows), rows)],
            fsem.at[0, d],
            fsem.at[1, d],
            {"seq": seq_peer(d)},
        )
        copy.start()
        feat_copies.append(copy)
    kg[pl.ds(pl.multiple_of(me * rows, rows), rows), :] = k_ref[...]
    ft[:, pl.ds(pl.multiple_of(me * rows, rows), rows)] = feat_ref[me]
    pre = pre_ref[...]
    act[...] = (pre * jax.nn.sigmoid(pre)).astype(BF16)
    sent = gather_finish(kg, ksem, key_copies)

    limit = limit_ref[0]

    def group(g, carry):
        keys = kg[:, pl.ds(pl.multiple_of(g * head, head), head)]
        kpos = kpos_ref[...]
        allowed = (kpos <= qpos_ref[...]) & (kpos < limit)
        column = jnp.zeros((1, n * rows), F32)
        for j in range(per_group):
            start = pl.multiple_of((g * per_group + j) * head, head)
            score = lax.dot_general(
                q_ref[:, pl.ds(start, head)],
                keys,
                (((1,), (1,)), ((), ())),
                preferred_element_type=F32,
            )
            masked = jnp.where(allowed, score * scale, -1e30)
            top = jnp.max(masked, axis=1, keepdims=True)
            weights = jnp.exp(masked - top)
            denom = jnp.sum(weights, axis=1, keepdims=True)
            column += jnp.sum(weights * (live_col_ref[...] / denom), axis=0, keepdims=True)
        msum[g] = column
        return carry

    lax.fori_loop(0, heads, group, 0)
    for p in range(n):
        mp[p] = msum[:, 0, p * rows : (p + 1) * rows]
    mass_copies = []
    for d in range(1, n):
        copy = copy_to(
            mp.at[seq_peer(d)], mr.at[d], msem.at[0, d], msem.at[1, d], {"seq": seq_peer(d)}
        )
        copy.start()
        mass_copies.append(copy)
    wt = wt_ref[...]
    pred = (
        lax.dot_general(wt, act[...], (((1,), (1,)), ((), ())), preferred_element_type=F32)[:heads]
        + bias_ref[...]
    )
    mass = mp[me]
    for d in range(1, n):
        mass_copies[d - 1].wait_recv()
        mass = mass + mr[d]
    sent += mass_copies
    resid = ((pred - jnp.log1p(mass)) * live_row_ref[...] * norm).astype(BF16)
    resid32 = resid.astype(F32)
    resid_all = jnp.concatenate([resid32, jnp.zeros_like(resid32)], axis=0)
    resid_t = resid_all.T.astype(BF16)
    back = jnp.dot(resid_t, wt, preferred_element_type=F32)
    pre = pre_ref[...]
    sig = jax.nn.sigmoid(pre)
    delta[...] = (back * sig * (1.0 + pre * (1.0 - sig))).astype(BF16)
    delta_copies = gather_start(delta, dg, dsem)
    dg[pl.ds(pl.multiple_of(me * rows, rows), rows), :] = delta[...]

    out_term = jnp.dot(resid_all.astype(BF16), act[...], preferred_element_type=F32)
    width = hidden // n
    bias_sum = jnp.broadcast_to(jnp.sum(resid32, axis=1, keepdims=True), (heads, width))
    for p in range(n):
        otc[p, :heads] = out_term[:heads, p * width : (p + 1) * width]
        otc[p, heads:] = bias_sum
    first = []
    for d in range(1, n):
        copy = copy_to(
            otc.at[seq_peer(d)], otr.at[d], osem.at[0, d], osem.at[1, d], {"seq": seq_peer(d)}
        )
        copy.start()
        first.append(copy)
    small = otc[me]
    for d in range(1, n):
        first[d - 1].wait_recv()
        small = small + otr[d]
    obs[...] = small
    second = []
    for d in range(1, nb):
        copy = copy_to(
            obs, obr.at[d], bsem.at[0, d], bsem.at[1, d], {"batch": batch_peer(d)}
        )
        copy.start()
        second.append(copy)

    sent += gather_finish(dg, dsem, delta_copies)
    for copy in feat_copies:
        copy.wait_recv()
    part = cs.shape[1]
    chunks = []
    for d in range(1, nb):
        start = pl.multiple_of(batch_peer(d) * part, 16)
        cs[d] = jnp.dot(ft[pl.ds(start, part), :], dg[...], preferred_element_type=F32)
        copy = copy_to(
            cs.at[d], cr.at[d], csem.at[0, d], csem.at[1, d], {"batch": batch_peer(d)}
        )
        copy.start()
        chunks.append(copy)
    dbs[...] = jnp.dot(jnp.ones((8, n * rows), BF16), dg[...], preferred_element_type=F32)
    sums = []
    for d in range(1, nb):
        copy = copy_to(
            dbs, dbr.at[d], gsem.at[0, d], gsem.at[1, d], {"batch": batch_peer(d)}
        )
        copy.start()
        sums.append(copy)

    small = obs[...]
    for d in range(1, nb):
        second[d - 1].wait_recv()
        small = small + obr[d]
    ofin[me] = small
    third = []
    for d in range(1, n):
        copy = copy_to(
            ofin.at[me], ofin.at[me], hsem.at[0, d], hsem.at[1, d], {"seq": seq_peer(d)}
        )
        copy.start()
        third.append(copy)
    start = pl.multiple_of(mb * part, 16)
    total = jnp.dot(ft[pl.ds(start, part), :], dg[...], preferred_element_type=F32)
    for d in range(1, nb):
        chunks[d - 1].wait_recv()
        total = total + cr[d]
    grad_ref[...] = total
    grad_b = dbs[...]
    for d in range(1, nb):
        sums[d - 1].wait_recv()
        grad_b = grad_b + dbr[d]
    gb_ref[...] = grad_b
    for copy in third:
        copy.wait_recv()
    gw_ref[...] = ofin[...]
    for copy in sent + feat_copies + first + second + chunks + sums + third:
        copy.wait_send()


def on_device(queries, keys, values, lengths, block_pos, w_in, b_in, output_weight, output_bias):
    n = lax.axis_size("seq")
    nb = lax.axis_size("batch")
    q_rows = queries[0]
    k_rows = keys[0]
    v_rows = values[0]
    rows, kd = k_rows.shape
    heads = output_weight.shape[1]
    hidden = w_in.shape[1]
    feat = w_in.shape[0]
    cols = feat // n
    part = cols // nb
    scale = 1.0 / math.sqrt(kd // heads)
    norm = 1.0 / math.sqrt(nb * n * rows)
    order = block_pos[0]
    offsets = jnp.arange(rows, dtype=jnp.int32)
    key_pos = (order[:, None] * rows + offsets[None, :]).reshape(1, -1)
    mine = lax.axis_index("seq")
    query_pos = lax.dynamic_index_in_dim(order, mine, 0, keepdims=False) * rows + offsets
    live = (query_pos < lengths[0]).astype(F32)
    features = jnp.concatenate([q_rows, k_rows, v_rows], axis=1)
    pre = jnp.dot(features, w_in, preferred_element_type=F32) + b_in
    turned = features.T.reshape(n, cols, rows)
    wt = jnp.pad(output_weight.T, ((0, heads), (0, 0)))
    vmem = pl.BlockSpec(memory_space=pltpu.VMEM)
    total = n * rows
    width = hidden // n
    grad, gb, gw = pl.pallas_call(
        functools.partial(kernel, n, nb, norm, scale),
        out_shape=(
            jax.ShapeDtypeStruct((part, hidden), F32),
            jax.ShapeDtypeStruct((8, hidden), F32),
            jax.ShapeDtypeStruct((n, 2 * heads, width), F32),
        ),
        in_specs=[vmem] * 10 + [pl.BlockSpec(memory_space=pltpu.SMEM)],
        out_specs=(vmem, vmem, vmem),
        scratch_shapes=[
            pltpu.VMEM((total, kd), BF16),
            pltpu.VMEM((cols, total), BF16),
            pltpu.VMEM((rows, hidden), BF16),
            pltpu.VMEM((heads, 1, total), F32),
            pltpu.VMEM((n, heads, rows), F32),
            pltpu.VMEM((n, heads, rows), F32),
            pltpu.VMEM((rows, hidden), BF16),
            pltpu.VMEM((total, hidden), BF16),
            pltpu.VMEM((n, 2 * heads, width), F32),
            pltpu.VMEM((n, 2 * heads, width), F32),
            pltpu.VMEM((2 * heads, width), F32),
            pltpu.VMEM((nb, 2 * heads, width), F32),
            pltpu.VMEM((n, 2 * heads, width), F32),
            pltpu.VMEM((8, hidden), F32),
            pltpu.VMEM((nb, 8, hidden), F32),
            pltpu.VMEM((nb, part, hidden), F32),
            pltpu.VMEM((nb, part, hidden), F32),
            pltpu.SemaphoreType.DMA((4, n)),
            pltpu.SemaphoreType.DMA((2, n)),
            pltpu.SemaphoreType.DMA((2, n)),
            pltpu.SemaphoreType.DMA((4, n)),
            pltpu.SemaphoreType.DMA((2, n)),
            pltpu.SemaphoreType.DMA((2, nb)),
            pltpu.SemaphoreType.DMA((2, nb)),
            pltpu.SemaphoreType.DMA((2, n)),
            pltpu.SemaphoreType.DMA((2, nb)),
        ],
        compiler_params=pltpu.CompilerParams(
            collective_id=0, has_side_effects=True, vmem_limit_bytes=60 * 1024 * 1024
        ),
    )(
        q_rows,
        k_rows,
        turned,
        pre,
        wt,
        output_bias[:, None],
        key_pos,
        query_pos[:, None],
        live[:, None],
        live[None, :],
        lengths,
    )
    weight_grad = jnp.moveaxis(gw[:, :heads], 0, 1).reshape(heads, hidden).T
    return (grad, gb[0], weight_grad, gw[0, heads:, 0])


def solution(mesh):
    return jax.shard_map(
        on_device,
        mesh=mesh,
        in_specs=(
            P("batch", "seq", None),
            P("batch", "seq", None),
            P("batch", "seq", None),
            P("batch"),
            P("batch", None),
            P(),
            P(),
            P(),
            P(),
        ),
        out_specs=(P(("seq", "batch"), None), P(), P(), P()),
        check_vma=False,
    )
```

time: 456 us -> 173 us (0.38)
  waiting for transfers between devices: 296 us -> 0 us
  Pallas kernels: 0 us -> 149 us
  matrix products: 72.3 us -> 7.29 us
  blocking collectives: 41 us -> 0 us
  between operations: 14.5 us -> 1.37 us
  other arithmetic: 15.1 us -> 6.62 us
  local copies, waits for them, and re-layouts: 15.2 us -> 9.03 us
    reduce_scatter x2 -> x0, waiting for transfers between devices: 254 us -> none  [the longest x1 201 us: on_device(): lax.psum_scatter(term, ('seq', 'batch'), scatter_dimension=0, tiled=True)]
    pallas_call x0 -> x1, Pallas kernels: none -> 149 us  [on_device(): pl.pallas_call(functools.partial(kernel, n, nb, norm, scale), out_shape=(...]
    all_gather x1 -> x0, waiting for transfers between devices: 41.6 us -> none  [on_device(): every_key = lax.all_gather(k_rows, 'seq', axis=0, tiled=True)]
    psum x1 -> x0, blocking collectives: 41 us -> none  [on_device(): lax.psum((jnp.sum(delta.astype(jnp.float32), axis=0), out_term, jnp.sum(r...]
    div x8 -> x0, matrix products: 27.3 us -> none  [group_mass(): share = weights / denom * query_live[None, :, None]]
    sub x8 -> x0, matrix products: 23.8 us -> none  [group_mass(): weights = jnp.where(allowed[None], jnp.exp(masked - top), 0.0)]
    dot_general x5 -> x1, matrix products: 21.2 us -> 7.29 us  [on_device(): pre = jnp.dot(features, w_in, preferred_element_type=F32) + b_in]
    dynamic_update_slice x8 -> x0, local copies, waits for them, and re-layouts: 11.2 us -> none  [group_mass(): return lax.dynamic_update_index_in_dim(sums, column, index, 0)]
  transfers between devices with their start and end apart: 3 -> 0, of which waited for: 3 -> 0; matrix products, arithmetic and copies ran while one was open for 3% -> 0% of each run, Pallas kernels for 0% -> 0%
where the time goes in v1:
time: 173 us
  Pallas kernels  149 us (86%)
  local copies, waits for them, and re-layouts  9.03 us (5%)
  matrix products  7.29 us (4%)
  other arithmetic  6.62 us (4%)
    pallas_call x1, Pallas kernels, on_device(): pl.pallas_call(functools.partial(kernel, n, nb, norm, scale), out_shape=(...  149 us
    dot_general x1, matrix products, on_device(): pre = jnp.dot(features, w_in, preferred_element_type=F32) + b_in  7.29 us

profile of v1, /device:TPU:0, one launch (start us, length us, event | category | flops | bytes accessed | tf_op | source)
XLA Modules:
  0.0 172.9 jit_solution(9912907103791450396)
XLA Ops:
  0.6 0.0 copy-start
  0.6 0.0 copy-start.1
  0.7 0.0 copy-start.2
  0.7 0.0 copy-start.5
  0.7 1.6 fusion
  2.3 1.6 copy.17
  3.9 0.0 copy-done
  3.9 0.0 copy-done.1
  3.9 0.0 copy-done.2
  3.9 0.0 copy-done.5
  3.9 0.0 copy-start.3
  3.9 0.0 copy-start.4
  3.9 0.0 copy-start.6
  3.9 7.3 %convolution_add_fusion.pre_ref = f32[128,1024]{1,0:T(8,128)} fusion(bf16[6144,1024]{1,0:T(8,128)(2,1)} %param.14, bf16[128,1024]{1,0:T(8,128)(2,1)S(1)} %bitcast.31, bf16[128,1024]{1,0:T(8,128)(2,1)S(1)} %bitcast.29, bf16[128,4096]{1,0:T(8,128)(2,1)S(1)} %bitcast.26, f32[1024]{0:T(1024)S(1)} %copy-done.5), kind=kOutput, calls=%fused_computation.1 | convolution fusion | flops 1615462400 | bytes 14684160 | tf_op jit(solution)/shard_map/dot_general | solution.py:305
  11.2 0.0 copy-done.3
  11.2 0.6 pad.4.wt_ref
  11.8 0.0 copy-done.4
  11.8 0.7 copy.19.bias_ref
  12.5 0.0 copy-done.6
  12.5 0.7 iota_add_fusion.1
  13.2 0.6 fusion.2
  13.8 1.3 iota_add_fusion.qpos_ref
  15.7 1.3 compare_convert_fusion.live_col_ref
  17.0 1.2 compare_convert_fusion.1.live_row_ref
  18.2 148.6 %shard_map.120 = (f32[192,1024]{1,0:T(8,128)}, f32[8,1024]{1,0:T(8,128)}, f32[8,16,128]{2,1,0:T(8,128)}) custom-call(bf16[128,4096]{1,0:T(8,128)(2,1)} %bitcast.25, bf16[128,1024]{1,0:T(8,128)(2,1)} %bitcast.28, bf16[8,768,128]{2,1,0:T(8,128)(2,1)} %bitcast.23, f32[128,1024]{1,0:T(8,128)} %convolution_add_fusion.pre_ref, bf16[16,1024]{1,0:T(8,128)(2,1)} %pad.4.wt_ref, ...), custom_call_target="tpu_custom_call" | custom-call | tf_op jit(solution)/shard_map/pallas_call | solution.py:311
  166.8 1.4 slice.9
  168.2 1.4 slice_bitcast_fusion
  169.5 1.3 slice_reduce_fusion
  170.8 2.1 %copy.22 = f32[192,1024]{1,0:T(8,128)} copy(f32[192,1024]{1,0:T(8,128)} %get-tuple-element.14) | data formatting | bytes 1572864
  (1 shorter events, 0.0 us)
Async XLA Ops:
  0.6 3.2 %copy-start = (bf16[1,128,4096]{2,1,0:T(8,128)(2,1)S(1)}, bf16[1,128,4096]{2,1,0:T(8,128)(2,1)}, u32[]{:S(2)}) copy-start(bf16[1,128,4096]{2,1,0:T(8,128)(2,1)} %param.9) | copy-start | bytes 3145732
  0.6 3.2 %copy-start.1 = (bf16[1,128,1024]{2,1,0:T(8,128)(2,1)S(1)}, bf16[1,128,1024]{2,1,0:T(8,128)(2,1)}, u32[]{:S(2)}) copy-start(bf16[1,128,1024]{2,1,0:T(8,128)(2,1)} %param.10) | copy-start | bytes 786436
  0.7 3.2 %copy-start.2 = (bf16[1,128,1024]{2,1,0:T(8,128)(2,1)S(1)}, bf16[1,128,1024]{2,1,0:T(8,128)(2,1)}, u32[]{:S(2)}) copy-start(bf16[1,128,1024]{2,1,0:T(8,128)(2,1)} %param.11) | copy-start | bytes 786436
  0.7 3.2 %copy-start.5 = (f32[1024]{0:T(1024)S(1)}, f32[1024]{0:T(1024)}, u32[]{:S(2)}) copy-start(f32[1024]{0:T(1024)} %param.15) | copy-start | bytes 12292
  3.9 7.3 %copy-start.3 = (bf16[1024,8]{0,1:T(8,128)(2,1)S(1)}, bf16[1024,8]{0,1:T(8,128)(2,1)}, u32[]{:S(2)}) copy-start(bf16[1024,8]{0,1:T(8,128)(2,1)} %param.16) | copy-start | bytes 49156
  3.9 7.9 %copy-start.4 = (f32[8]{0:T(128)S(1)}, f32[8]{0:T(128)}, u32[]{:S(2)}) copy-start(f32[8]{0:T(128)} %param.17) | copy-start | bytes 100
  3.9 8.6 %copy-start.6 = (s32[1,8]{1,0:T(1,128)S(1)}, s32[1,8]{1,0:T(1,128)}, u32[]{:S(2)}) copy-start(s32[1,8]{1,0:T(1,128)} %param.13) | copy-start | bytes 100

commit v2 on v1

--- a/solution.py
+++ b/solution.py
@@ -31,18 +31,17 @@
     scale,
     q_ref,
     k_ref,
-    feat_ref,
-    pre_ref,
+    v_ref,
+    w_ref,
+    b_ref,
     wt_ref,
     bias_ref,
-    kpos_ref,
-    qpos_ref,
-    live_col_ref,
-    live_row_ref,
+    order_ref,
     limit_ref,
     grad_ref,
     gb_ref,
     gw_ref,
+    ob_ref,
     kg,
     ft,
     act,
@@ -69,6 +68,11 @@
     gsem,
     hsem,
     csem,
+    turned,
+    weights_in,
+    pre_ref,
+    mask,
+    wsem,
 ):
     me = lax.axis_index("seq")
     mb = lax.axis_index("batch")
@@ -77,6 +81,8 @@
     head = kd // heads
     per_group = q_ref.shape[1] // kd
     hidden = pre_ref.shape[1]
+    load = pltpu.make_async_copy(w_ref, weights_in, wsem)
+    load.start()
     inner = 2
     outer = n // inner
     mo = me // inner
@@ -133,28 +139,69 @@
 
     key_copies = gather_start(k_ref, kg, ksem)
     feat_copies = []
-    for d in range(1, n):
-        copy = copy_to(
-            feat_ref.at[seq_peer(d)],
-            ft.at[:, pl.ds(pl.multiple_of(me * rows, rows), rows)],
-            fsem.at[0, d],
-            fsem.at[1, d],
-            {"seq": seq_peer(d)},
-        )
-        copy.start()
-        feat_copies.append(copy)
+    cols = ft.shape[0]
+
+    def send_features(first, last):
+        for d in range(first, last):
+            copy = copy_to(
+                turned.at[pl.ds(pl.multiple_of(seq_peer(d) * cols, 16), cols)],
+                ft.at[:, pl.ds(pl.multiple_of(me * rows, rows), rows)],
+                fsem.at[0, d],
+                fsem.at[1, d],
+                {"seq": seq_peer(d)},
+            )
+            copy.start()
+            feat_copies.append(copy)
+
     kg[pl.ds(pl.multiple_of(me * rows, rows), rows), :] = k_ref[...]
-    ft[:, pl.ds(pl.multiple_of(me * rows, rows), rows)] = feat_ref[me]
-    pre = pre_ref[...]
-    act[...] = (pre * jax.nn.sigmoid(pre)).astype(BF16)
+    base = 0
+    for ref in (q_ref, k_ref, v_ref):
+
+        def turn(c, carry, ref=ref, base=base):
+            tile = ref[:, pl.ds(pl.multiple_of(c * head, head), head)]
+            turned[pl.ds(pl.multiple_of(base + c * head, head), head), :] = tile.T
+            return carry
+
+        lax.fori_loop(0, ref.shape[1] // head, turn, 0)
+        base += ref.shape[1]
+    load.wait()
+    tile_width = hidden // 4
+
+    def project(c, carry):
+        span = pl.ds(pl.multiple_of(c * tile_width, tile_width), tile_width)
+        value = b_ref[:, span]
+        base = 0
+        for ref in (q_ref, k_ref, v_ref):
+            depth = ref.shape[1]
+            value = value + jnp.dot(
+                ref[...], weights_in[base : base + depth, span], preferred_element_type=F32
+            )
+            base += depth
+        pre_ref[:, span] = value
+        act[:, span] = (value * jax.nn.sigmoid(value)).astype(BF16)
+        return carry
+
+    lax.fori_loop(0, 4, project, 0)
+    ft[:, pl.ds(pl.multiple_of(me * rows, rows), rows)] = turned[
+        pl.ds(pl.multiple_of(me * cols, 16), cols), :
+    ]
     sent = gather_finish(kg, ksem, key_copies)
+    early = n // 2
+    send_features(1, early)
 
     limit = limit_ref[0]
+    lane = lax.broadcasted_iota(jnp.int32, (1, rows), 1)
+    key_pos = jnp.concatenate([lane + order_ref[0, p] * rows for p in range(n)], axis=1)
+    query_start = order_ref[0, me] * rows
+    query_pos = lax.broadcasted_iota(jnp.int32, (rows, 1), 0) + query_start
+    live_col = (query_pos < limit).astype(F32)
+    live_row = (lane + query_start < limit).astype(F32)
+    allowed = (key_pos <= query_pos) & (key_pos < limit)
+    mask[...] = jnp.where(allowed, 0.0, -1e30)
 
     def group(g, carry):
         keys = kg[:, pl.ds(pl.multiple_of(g * head, head), head)]
-        kpos = kpos_ref[...]
-        allowed = (kpos <= qpos_ref[...]) & (kpos < limit)
+        hide = mask[...]
         column = jnp.zeros((1, n * rows), F32)
         for j in range(per_group):
             start = pl.multiple_of((g * per_group + j) * head, head)
@@ -164,11 +211,11 @@
                 (((1,), (1,)), ((), ())),
                 preferred_element_type=F32,
             )
-            masked = jnp.where(allowed, score * scale, -1e30)
+            masked = jnp.where(hide < 0.0, hide, score * scale)
             top = jnp.max(masked, axis=1, keepdims=True)
             weights = jnp.exp(masked - top)
             denom = jnp.sum(weights, axis=1, keepdims=True)
-            column += jnp.sum(weights * (live_col_ref[...] / denom), axis=0, keepdims=True)
+            column += jnp.sum(weights * (live_col / denom), axis=0, keepdims=True)
         msum[g] = column
         return carry
 
@@ -192,7 +239,7 @@
         mass_copies[d - 1].wait_recv()
         mass = mass + mr[d]
     sent += mass_copies
-    resid = ((pred - jnp.log1p(mass)) * live_row_ref[...] * norm).astype(BF16)
+    resid = ((pred - jnp.log1p(mass)) * live_row * norm).astype(BF16)
     resid32 = resid.astype(F32)
     resid_all = jnp.concatenate([resid32, jnp.zeros_like(resid32)], axis=0)
     resid_t = resid_all.T.astype(BF16)
@@ -201,6 +248,7 @@
     sig = jax.nn.sigmoid(pre)
     delta[...] = (back * sig * (1.0 + pre * (1.0 - sig))).astype(BF16)
     delta_copies = gather_start(delta, dg, dsem)
+    send_features(early, n)
     dg[pl.ds(pl.multiple_of(me * rows, rows), rows), :] = delta[...]
 
     out_term = jnp.dot(resid_all.astype(BF16), act[...], preferred_element_type=F32)
@@ -273,10 +321,11 @@
     for d in range(1, nb):
         sums[d - 1].wait_recv()
         grad_b = grad_b + dbr[d]
-    gb_ref[...] = grad_b
+    gb_ref[...] = grad_b[:1]
     for copy in third:
         copy.wait_recv()
-    gw_ref[...] = ofin[...]
+    gw_ref[...] = jnp.concatenate([ofin[p, :heads] for p in range(n)], axis=1).T
+    ob_ref[...] = ofin[0, heads:, :1]
     for copy in sent + feat_copies + first + second + chunks + sums + third:
         copy.wait_send()
 
@@ -295,28 +344,23 @@
     part = cols // nb
     scale = 1.0 / math.sqrt(kd // heads)
     norm = 1.0 / math.sqrt(nb * n * rows)
-    order = block_pos[0]
-    offsets = jnp.arange(rows, dtype=jnp.int32)
-    key_pos = (order[:, None] * rows + offsets[None, :]).reshape(1, -1)
-    mine = lax.axis_index("seq")
-    query_pos = lax.dynamic_index_in_dim(order, mine, 0, keepdims=False) * rows + offsets
-    live = (query_pos < lengths[0]).astype(F32)
-    features = jnp.concatenate([q_rows, k_rows, v_rows], axis=1)
-    pre = jnp.dot(features, w_in, preferred_element_type=F32) + b_in
-    turned = features.T.reshape(n, cols, rows)
     wt = jnp.pad(output_weight.T, ((0, heads), (0, 0)))
     vmem = pl.BlockSpec(memory_space=pltpu.VMEM)
     total = n * rows
     width = hidden // n
-    grad, gb, gw = pl.pallas_call(
+    grad, gb, gw, ob = pl.pallas_call(
         functools.partial(kernel, n, nb, norm, scale),
         out_shape=(
             jax.ShapeDtypeStruct((part, hidden), F32),
-            jax.ShapeDtypeStruct((8, hidden), F32),
-            jax.ShapeDtypeStruct((n, 2 * heads, width), F32),
+            jax.ShapeDtypeStruct((1, hidden), F32),
+            jax.ShapeDtypeStruct((hidden, heads), F32),
+            jax.ShapeDtypeStruct((heads, 1), F32),
         ),
-        in_specs=[vmem] * 10 + [pl.BlockSpec(memory_space=pltpu.SMEM)],
-        out_specs=(vmem, vmem, vmem),
+        in_specs=[vmem] * 3
+        + [pl.BlockSpec(memory_space=pl.ANY)]
+        + [vmem] * 3
+        + [pl.BlockSpec(memory_space=pltpu.SMEM)] * 2,
+        out_specs=(vmem, vmem, vmem, vmem),
         scratch_shapes=[
             pltpu.VMEM((total, kd), BF16),
             pltpu.VMEM((cols, total), BF16),
@@ -344,6 +388,11 @@
             pltpu.SemaphoreType.DMA((2, nb)),
             pltpu.SemaphoreType.DMA((2, n)),
             pltpu.SemaphoreType.DMA((2, nb)),
+            pltpu.VMEM((feat, rows), BF16),
+            pltpu.VMEM((feat, hidden), BF16),
+            pltpu.VMEM((rows, hidden), F32),
+            pltpu.VMEM((rows, total), F32),
+            pltpu.SemaphoreType.DMA,
         ],
         compiler_params=pltpu.CompilerParams(
             collective_id=0, has_side_effects=True, vmem_limit_bytes=60 * 1024 * 1024
@@ -351,18 +400,15 @@
     )(
         q_rows,
         k_rows,
-        turned,
-        pre,
+        v_rows,
+        w_in,
+        b_in[None, :],
         wt,
         output_bias[:, None],
-        key_pos,
-        query_pos[:, None],
-        live[:, None],
-        live[None, :],
+        block_pos,
         lengths,
     )
-    weight_grad = jnp.moveaxis(gw[:, :heads], 0, 1).reshape(heads, hidden).T
-    return (grad, gb[0], weight_grad, gw[0, heads:, 0])
+    return (grad, gb[0], gw, ob[:, 0])
 
 
 def solution(mesh):

time: 173 us -> 178 us (1.029)
  Pallas kernels: 149 us -> 167 us
  matrix products: 7.29 us -> 0 us
  other arithmetic: 6.62 us -> 1.3 us
    pallas_call x1, Pallas kernels: 149 us -> 167 us  [on_device(): pl.pallas_call(functools.partial(kernel, n, nb, norm, scale), out_shape=(...]
    dot_general x1 -> x0, matrix products: 7.29 us -> none  [on_device(): pre = jnp.dot(features, w_in, preferred_element_type=F32) + b_in]
    unnamed x15 -> x3, local copies, waits for them, and re-layouts: 2.13 us -> 5.18 us
    transpose x2 -> x0, local copies, waits for them, and re-layouts: 2.95 us -> none  [the longest x1 1.58 us: on_device(): turned = features.T.reshape(n, cols, rows)]
    slice x2 -> x0, local copies, waits for them, and re-layouts: 2.66 us -> none  [on_device(): return (grad, gb[0], weight_grad, gw[0, heads:, 0])]
    convert_element_type x2 -> x0, other arithmetic: 2.51 us -> none  [on_device(): live = (query_pos < lengths[0]).astype(F32)]
    add x2 -> x0, other arithmetic: 1.93 us -> none  [the longest x1 1.27 us: on_device(): lax.dynamic_index_in_dim(order, mine, 0, keepdims=False) * rows + offsets]
where the time goes in v2:
time: 178 us
  Pallas kernels  167 us (94%)
  local copies, waits for them, and re-layouts  7.84 us (4%)
    pallas_call x1, Pallas kernels, on_device(): pl.pallas_call(functools.partial(kernel, n, nb, norm, scale), out_shape=(...  167 us
    unnamed x3, local copies, waits for them, and re-layouts  5.18 us

profile of v2, /device:TPU:0, one launch (start us, length us, event | category | flops | bytes accessed | tf_op | source)
XLA Modules:
  0.0 177.7 jit_solution(8248026927687458263)
XLA Ops:
  1.3 1.3 copy.15.bias_ref
  2.6 1.3 pad.4.wt_ref
  3.9 167.3 %shard_map.120 = (f32[192,1024]{1,0:T(8,128)}, f32[1,1024]{1,0:T(1,128)}, f32[1024,8]{1,0:T(8,128)}, f32[8,1]{1,0:T(8,128)}) custom-call(bf16[128,4096]{1,0:T(8,128)(2,1)} %bitcast.7, bf16[128,1024]{1,0:T(8,128)(2,1)} %bitcast.8, bf16[128,1024]{1,0:T(8,128)(2,1)} %bitcast.9, bf16[6144,1024]{1,0:T(8,128)(2,1)} %w_ref.1, f32[1,1024]{1,0:T(1,128)} %bitcast.11, ...), custom_call_target="tpu_custom_call" | custom-call | tf_op jit(solution)/shard_map/pallas_call | solution.py:351
  171.2 1.3 reduce
  172.5 1.8 %copy.16 = f32[1024,8]{0,1:T(8,128)} copy(f32[1024,8]{1,0:T(8,128)} %get-tuple-element.18) | data formatting | bytes 65536
  174.4 2.1 %copy.20 = f32[192,1024]{1,0:T(8,128)} copy(f32[192,1024]{1,0:T(8,128)} %get-tuple-element.24) | data formatting | bytes 1572864
  176.4 1.3 copy.21

commit v3 on v2

--- a/solution.py
+++ b/solution.py
@@ -10,6 +10,7 @@
 
 F32 = jnp.float32
 BF16 = jnp.bfloat16
+PIECES = 2
 MESH = pl.DeviceIdType.MESH
 
 
@@ -72,6 +73,9 @@
     weights_in,
     pre_ref,
     mask,
+    ns,
+    nr,
+    nsem,
     wsem,
 ):
     me = lax.axis_index("seq")
@@ -186,7 +190,7 @@
         pl.ds(pl.multiple_of(me * cols, 16), cols), :
     ]
     sent = gather_finish(kg, ksem, key_copies)
-    early = n // 2
+    early = n
     send_features(1, early)
 
     limit = limit_ref[0]
@@ -246,10 +250,15 @@
     back = jnp.dot(resid_t, wt, preferred_element_type=F32)
     pre = pre_ref[...]
     sig = jax.nn.sigmoid(pre)
-    delta[...] = (back * sig * (1.0 + pre * (1.0 - sig))).astype(BF16)
-    delta_copies = gather_start(delta, dg, dsem)
-    send_features(early, n)
-    dg[pl.ds(pl.multiple_of(me * rows, rows), rows), :] = delta[...]
+    slope = (back * sig * (1.0 + pre * (1.0 - sig))).astype(BF16)
+    piece = hidden // PIECES
+    delta_copies = []
+    for h in range(PIECES):
+        delta[h] = slope[:, h * piece : (h + 1) * piece]
+        delta_copies.append(gather_start(delta.at[h], dg.at[h], dsem.at[h]))
+        if h == 0:
+            send_features(early, n)
+        dg[h, pl.ds(pl.multiple_of(me * rows, rows), rows), :] = delta[h]
 
     out_term = jnp.dot(resid_all.astype(BF16), act[...], preferred_element_type=F32)
     width = hidden // n
@@ -277,20 +286,54 @@
         copy.start()
         second.append(copy)
 
-    sent += gather_finish(dg, dsem, delta_copies)
-    for copy in feat_copies:
-        copy.wait_recv()
-    part = cs.shape[1]
+    part = cr.shape[2]
+    bo = mb // inner
+    bi = mb % inner
+    bouter = nb // inner
+    twin = bo * inner + (inner - 1 - bi)
+
+    def term(h, owner):
+        start = pl.multiple_of(owner * part, 16)
+        return jnp.dot(ft[pl.ds(start, part), :], dg[h], preferred_element_type=F32)
+
     chunks = []
-    for d in range(1, nb):
-        start = pl.multiple_of(batch_peer(d) * part, 16)
-        cs[d] = jnp.dot(ft[pl.ds(start, part), :], dg[...], preferred_element_type=F32)
-        copy = copy_to(
-            cs.at[d], cr.at[d], csem.at[0, d], csem.at[1, d], {"batch": batch_peer(d)}
-        )
-        copy.start()
-        chunks.append(copy)
-    dbs[...] = jnp.dot(jnp.ones((8, n * rows), BF16), dg[...], preferred_element_type=F32)
+    near = []
+    for h in range(PIECES):
+        sent += gather_finish(dg.at[h], dsem.at[h], delta_copies[h])
+        if h == 0:
+            for copy in feat_copies:
+                copy.wait_recv()
+        swaps = []
+        for e in range(bouter):
+            ahead = lax.rem(bo + 1 + e, bouter)
+            ns[h, e] = term(h, ahead * inner + (inner - 1 - bi))
+            copy = copy_to(
+                ns.at[h, e], nr.at[h, e], nsem.at[0, h, e], nsem.at[1, h, e], {"batch": twin}
+            )
+            copy.start()
+            swaps.append(copy)
+        near += swaps
+        for e in range(bouter):
+            ahead = lax.rem(bo + 1 + e, bouter)
+            value = term(h, ahead * inner + bi)
+            swaps[e].wait_recv()
+            value = value + nr[h, e]
+            if e == bouter - 1:
+                grad_ref[:, h * piece : (h + 1) * piece] = value
+            else:
+                cs[h, e] = value
+                copy = copy_to(
+                    cs.at[h, e],
+                    cr.at[h, e],
+                    csem.at[0, h, e],
+                    csem.at[1, h, e],
+                    {"batch": ahead * inner + bi},
+                )
+                copy.start()
+                chunks.append((h, e, copy))
+        dbs[:, h * piece : (h + 1) * piece] = jnp.dot(
+            jnp.ones((8, n * rows), BF16), dg[h], preferred_element_type=F32
+        )
     sums = []
     for d in range(1, nb):
         copy = copy_to(
@@ -311,12 +354,9 @@
         )
         copy.start()
         third.append(copy)
-    start = pl.multiple_of(mb * part, 16)
-    total = jnp.dot(ft[pl.ds(start, part), :], dg[...], preferred_element_type=F32)
-    for d in range(1, nb):
-        chunks[d - 1].wait_recv()
-        total = total + cr[d]
-    grad_ref[...] = total
+    for h, e, copy in chunks:
+        copy.wait_recv()
+        grad_ref[:, h * piece : (h + 1) * piece] += cr[h, e]
     grad_b = dbs[...]
     for d in range(1, nb):
         sums[d - 1].wait_recv()
@@ -326,7 +366,7 @@
         copy.wait_recv()
     gw_ref[...] = jnp.concatenate([ofin[p, :heads] for p in range(n)], axis=1).T
     ob_ref[...] = ofin[0, heads:, :1]
-    for copy in sent + feat_copies + first + second + chunks + sums + third:
+    for copy in sent + feat_copies + first + second + near + sums + third + [c[2] for c in chunks]:
         copy.wait_send()
 
 
@@ -368,8 +408,8 @@
             pltpu.VMEM((heads, 1, total), F32),
             pltpu.VMEM((n, heads, rows), F32),
             pltpu.VMEM((n, heads, rows), F32),
-            pltpu.VMEM((rows, hidden), BF16),
-            pltpu.VMEM((total, hidden), BF16),
+            pltpu.VMEM((PIECES, rows, hidden // PIECES), BF16),
+            pltpu.VMEM((PIECES, total, hidden // PIECES), BF16),
             pltpu.VMEM((n, 2 * heads, width), F32),
             pltpu.VMEM((n, 2 * heads, width), F32),
             pltpu.VMEM((2 * heads, width), F32),
@@ -377,21 +417,24 @@
             pltpu.VMEM((n, 2 * heads, width), F32),
             pltpu.VMEM((8, hidden), F32),
             pltpu.VMEM((nb, 8, hidden), F32),
-            pltpu.VMEM((nb, part, hidden), F32),
-            pltpu.VMEM((nb, part, hidden), F32),
+            pltpu.VMEM((PIECES, nb // 2, part, hidden // PIECES), F32),
+            pltpu.VMEM((PIECES, nb // 2, part, hidden // PIECES), F32),
             pltpu.SemaphoreType.DMA((4, n)),
             pltpu.SemaphoreType.DMA((2, n)),
             pltpu.SemaphoreType.DMA((2, n)),
-            pltpu.SemaphoreType.DMA((4, n)),
+            pltpu.SemaphoreType.DMA((PIECES, 4, n)),
             pltpu.SemaphoreType.DMA((2, n)),
             pltpu.SemaphoreType.DMA((2, nb)),
             pltpu.SemaphoreType.DMA((2, nb)),
             pltpu.SemaphoreType.DMA((2, n)),
-            pltpu.SemaphoreType.DMA((2, nb)),
+            pltpu.SemaphoreType.DMA((2, PIECES, nb)),
             pltpu.VMEM((feat, rows), BF16),
             pltpu.VMEM((feat, hidden), BF16),
             pltpu.VMEM((rows, hidden), F32),
             pltpu.VMEM((rows, total), F32),
+            pltpu.VMEM((PIECES, nb // 2, part, hidden // PIECES), F32),
+            pltpu.VMEM((PIECES, nb // 2, part, hidden // PIECES), F32),
+            pltpu.SemaphoreType.DMA((2, PIECES, nb)),
             pltpu.SemaphoreType.DMA,
         ],
         compiler_params=pltpu.CompilerParams(

time: 178 us -> 151 us (0.85)
  Pallas kernels: 167 us -> 141 us
    pallas_call x1, Pallas kernels: 167 us -> 141 us  [on_device(): pl.pallas_call(functools.partial(kernel, n, nb, norm, scale), out_shape=(...]
where the time goes in v3:
time: 151 us
  Pallas kernels  141 us (93%)
  local copies, waits for them, and re-layouts  7.84 us (5%)
    pallas_call x1, Pallas kernels, on_device(): pl.pallas_call(functools.partial(kernel, n, nb, norm, scale), out_shape=(...  141 us
    unnamed x3, local copies, waits for them, and re-layouts  5.18 us

profile of v3, /device:TPU:0, one launch (start us, length us, event | category | flops | bytes accessed | tf_op | source)
XLA Modules:
  0.0 151.0 jit_solution(15473080030956260463)
XLA Ops:
  1.3 1.3 copy.15.bias_ref
  2.6 1.3 pad.4.wt_ref
  3.9 140.6 %shard_map.120 = (f32[192,1024]{1,0:T(8,128)}, f32[1,1024]{1,0:T(1,128)}, f32[1024,8]{1,0:T(8,128)}, f32[8,1]{1,0:T(8,128)}) custom-call(bf16[128,4096]{1,0:T(8,128)(2,1)} %bitcast.7, bf16[128,1024]{1,0:T(8,128)(2,1)} %bitcast.8, bf16[128,1024]{1,0:T(8,128)(2,1)} %bitcast.9, bf16[6144,1024]{1,0:T(8,128)(2,1)} %w_ref.1, f32[1,1024]{1,0:T(1,128)} %bitcast.11, ...), custom_call_target="tpu_custom_call" | custom-call | tf_op jit(solution)/shard_map/pallas_call | solution.py:391
  144.5 1.3 reduce
  145.8 1.8 %copy.16 = f32[1024,8]{0,1:T(8,128)} copy(f32[1024,8]{1,0:T(8,128)} %get-tuple-element.18) | data formatting | bytes 65536
  147.7 2.1 %copy.20 = f32[192,1024]{1,0:T(8,128)} copy(f32[192,1024]{1,0:T(8,128)} %get-tuple-element.24) | data formatting | bytes 1572864
  149.8 1.3 copy.21

commit v4 on v3

--- a/solution.py
+++ b/solution.py
@@ -129,7 +129,7 @@
         copy.start()
         return copies, [copy]
 
-    def gather_finish(dst, sem, started):
+    def gather_finish(dst, sem, started, follow=None):
         direct, passed = started
         for d in range(1, outer):
             direct[d - 1].wait_recv()
@@ -137,6 +137,8 @@
             copy = copy_to(held, held, sem.at[2, d], sem.at[3, d], {"seq": pair})
             copy.start()
             passed.append(copy)
+        if follow is not None:
+            follow()
         for copy in passed:
             copy.wait_recv()
         return direct + passed
@@ -189,9 +191,7 @@
     ft[:, pl.ds(pl.multiple_of(me * rows, rows), rows)] = turned[
         pl.ds(pl.multiple_of(me * cols, 16), cols), :
     ]
-    sent = gather_finish(kg, ksem, key_copies)
-    early = n
-    send_features(1, early)
+    sent = gather_finish(kg, ksem, key_copies, lambda: send_features(1, n))
 
     limit = limit_ref[0]
     lane = lax.broadcasted_iota(jnp.int32, (1, rows), 1)
@@ -256,8 +256,6 @@
     for h in range(PIECES):
         delta[h] = slope[:, h * piece : (h + 1) * piece]
         delta_copies.append(gather_start(delta.at[h], dg.at[h], dsem.at[h]))
-        if h == 0:
-            send_features(early, n)
         dg[h, pl.ds(pl.multiple_of(me * rows, rows), rows), :] = delta[h]
 
     out_term = jnp.dot(resid_all.astype(BF16), act[...], preferred_element_type=F32)

time: 151 us -> 143 us (0.947)
  Pallas kernels: 141 us -> 132 us
    pallas_call x1, Pallas kernels: 141 us -> 132 us  [on_device(): pl.pallas_call(functools.partial(kernel, n, nb, norm, scale), out_shape=(...]
where the time goes in v4:
time: 143 us
  Pallas kernels  132 us (92%)
  local copies, waits for them, and re-layouts  7.84 us (5%)
    pallas_call x1, Pallas kernels, on_device(): pl.pallas_call(functools.partial(kernel, n, nb, norm, scale), out_shape=(...  132 us
    unnamed x3, local copies, waits for them, and re-layouts  5.18 us

profile of v4, /device:TPU:0, one launch (start us, length us, event | category | flops | bytes accessed | tf_op | source)
XLA Modules:
  0.0 142.7 jit_solution(13103464843395909159)
XLA Ops:
  1.3 1.3 copy.15.bias_ref
  2.6 1.3 pad.4.wt_ref
  3.9 132.3 %shard_map.120 = (f32[192,1024]{1,0:T(8,128)}, f32[1,1024]{1,0:T(1,128)}, f32[1024,8]{1,0:T(8,128)}, f32[8,1]{1,0:T(8,128)}) custom-call(bf16[128,4096]{1,0:T(8,128)(2,1)} %bitcast.7, bf16[128,1024]{1,0:T(8,128)(2,1)} %bitcast.8, bf16[128,1024]{1,0:T(8,128)(2,1)} %bitcast.9, bf16[6144,1024]{1,0:T(8,128)(2,1)} %w_ref.1, f32[1,1024]{1,0:T(1,128)} %bitcast.11, ...), custom_call_target="tpu_custom_call" | custom-call | tf_op jit(solution)/shard_map/pallas_call | solution.py:389
  136.2 1.3 reduce
  137.5 1.8 %copy.16 = f32[1024,8]{0,1:T(8,128)} copy(f32[1024,8]{1,0:T(8,128)} %get-tuple-element.18) | data formatting | bytes 65536
  139.4 2.1 %copy.20 = f32[192,1024]{1,0:T(8,128)} copy(f32[192,1024]{1,0:T(8,128)} %get-tuple-element.24) | data formatting | bytes 1572864
  141.5 1.3 copy.21
